TPU v7x, 32 devices: a whole 2x2x4 slice. The times are simulated.
32 devices in a mesh: mem: 8 (over y, x, core), patch: 4 (over z).
Axes of the slice: x: 2, y: 2, z: 4, core: 2. Of those that a mesh axis runs over, the one named last changes fastest.
Arguments:
- state: bfloat16 [1024, 16384], P('mem', 'patch'), may hold values from -6 to 6
- obs_ens: bfloat16 [1024, 8192], P('mem', 'patch'), may hold values from -6 to 6
- obs_values: float32 [8192], P('patch'), may hold values from -8 to 8
- obs_weight: float32 [8192], P('patch'), may hold values from 0.2 to 5
- counts: int32 [32], P('patch'), may hold values from 32 to 256
Outputs:
- analysis: bfloat16 [1024, 16384], P('mem', 'patch')
Inputs may be any that keep to these rules, and one draw needn't show every extreme that they name: Region r uses the first counts[r] of its 256 observations.
All inputs are finite; a program needn't handle non-finite values. Where the computation divides by a largest or mean magnitude, that divisor is 1e-20 or more.
Results may differ from a plain program's by a relative error of at most 0.0047.
Values may be sent and summed in bfloat16 or wider, within the bound.
A program may use at most 64 MiB of HBM per device.

v0:
```python
import math
import jax
import jax.numpy as jnp
from jax import lax
from jax.sharding import PartitionSpec as P

DEGREE = 7


def extended(cells, sides, width):
    for axis, dim in sides:
        count = lax.axis_size(axis)
        head = lax.slice_in_dim(cells, 0, width, axis=dim)
        tail = lax.slice_in_dim(cells, cells.shape[dim] - width, cells.shape[dim], axis=dim)
        cells = jnp.concatenate(
            [
                lax.ppermute(tail, axis, [(i, (i + 1) % count) for i in range(count)]),
                cells,
                lax.ppermute(head, axis, [((i + 1) % count, i) for i in range(count)]),
            ],
            axis=dim,
        )
    return cells


def root_curve(values):
    lifted = jnp.sqrt(1.0 + values)
    return -1.0 / (lifted * (1.0 + lifted))


def inverse_curve(values):
    return 1.0 / (1.0 + values)


def chebyshev(upper, curve):
    number = DEGREE + 1
    theta = (jnp.arange(number, dtype=jnp.float32) + 0.5) * (math.pi / number)
    nodes = upper * (jnp.cos(theta) + 1.0) * 0.5
    samples = curve(nodes)
    orders = jnp.arange(number, dtype=jnp.float32)
    table = jnp.cos(orders[:, None] * theta[None, :])
    coefs = 2.0 / number * jnp.sum(table * samples[None, :], axis=1)
    return coefs * jnp.where(orders == 0.0, 0.5, 1.0)


def clenshaw(block, matrix, coefs):
    nearer = coefs[DEGREE] * block
    farther = jnp.zeros_like(block)
    for order in range(DEGREE - 1, 0, -1):
        current = (
            coefs[order] * block
            + 2.0 * jnp.dot(nearer, matrix, precision=lax.Precision.HIGHEST)
            - farther
        )
        farther, nearer = (nearer, current)
    return coefs[0] * block + jnp.dot(nearer, matrix, precision=lax.Precision.HIGHEST) - farther


def cross_product(left, right):
    return lax.dot_general(
        left, right, (((0,), (0,)), ((), ())), preferred_element_type=jnp.float32
    )


def on_device(state, obs_ens, obs_values, obs_weight, counts):
    mem_index = lax.axis_index("mem")
    own = obs_ens.shape[1] // lax.axis_size("mem")
    half = own // 2
    values = lax.dynamic_slice_in_dim(obs_values, mem_index * own, own, 0)
    weights = lax.dynamic_slice_in_dim(obs_weight, mem_index * own, own, 0)
    count = lax.dynamic_slice_in_dim(counts, mem_index, 1, 0)[0]
    region_state, region_obs = (
        lax.all_to_all(state, "mem", split_axis=1, concat_axis=0, tiled=True),
        lax.all_to_all(obs_ens, "mem", split_axis=1, concat_axis=0, tiled=True),
    )
    members = region_obs.shape[0]
    full_obs = region_obs.astype(jnp.float32)
    obs_centre = jnp.mean(full_obs, axis=0)
    mask = (jnp.arange(own, dtype=jnp.int32) < count).astype(jnp.float32)
    root = jnp.sqrt(weights * mask)
    own_gains = ((full_obs - obs_centre[None, :]) * root[None, :]).astype(jnp.bfloat16)
    own_innov = (root * (values - obs_centre)).astype(jnp.bfloat16)
    stacked = jnp.concatenate([own_gains, own_innov[None, :]], axis=0)
    widened = extended(stacked, (("patch", 1),), half)
    gains = widened[:-1]
    innov = widened[-1].astype(jnp.float32)
    normal = cross_product(gains, gains) / (members - 1)
    upper = jnp.max(jnp.sum(jnp.abs(normal), axis=1)) + 1e-06
    shifted = normal * (2.0 / upper) - jnp.eye(normal.shape[0], dtype=jnp.float32)
    full = region_state.astype(jnp.float32)
    centre = jnp.mean(full, axis=0)
    spread = (full - centre[None, :]).astype(jnp.bfloat16)
    product = cross_product(spread, gains)
    mixed = clenshaw(product, shifted, chebyshev(upper, root_curve)).astype(jnp.bfloat16)
    mean_weights = clenshaw(innov[None, :], shifted, chebyshev(upper, inverse_curve))[0]
    mean_shift = jnp.dot(product, mean_weights, precision=lax.Precision.HIGHEST) / (members - 1)
    update = lax.dot_general(
        gains, mixed, (((1,), (1,)), ((), ())), preferred_element_type=jnp.float32
    ) / (members - 1)
    analysed = (full + mean_shift[None, :] + update).astype(jnp.bfloat16)
    return lax.all_to_all(analysed, "mem", split_axis=0, concat_axis=1, tiled=True)


def solution(mesh):
    placed = (P("mem", "patch"), P("mem", "patch"), P("patch"), P("patch"), P("patch"))
    return jax.shard_map(
        on_device, mesh=mesh, in_specs=placed, out_specs=P("mem", "patch"), check_vma=False
    )
```

profile of v0, /device:TPU:0, one launch (start us, length us, event | category | flops | bytes accessed | tf_op | source)
XLA Modules:
  0.0 93.4 jit_solution(3490035947268976717)
XLA Ops:
  0.0 0.0 copy-start.3
  0.0 2.1 %copy.15 = bf16[128,2048]{0,1:T(8,128)(2,1)} copy(bf16[128,2048]{1,0:T(8,128)(2,1)} %param.6) | data formatting | bytes 1048576 | tf_op args[1]
  2.1 5.2 %all-to-all-start.1 = ((bf16[128,8,256]{0,2,1:T(8,128)(2,1)}), bf16[128,8,256]{0,2,1:T(8,128)(2,1)S(1)}, u32[]{:S(2)}, u32[]{:S(2)}) async-start(bf16[128,8,256]{0,2,1:T(8,128)(2,1)} %bitcast.3), calls=%async_computation.1 | async-start | bytes 1048576 | tf_op jit(solution)/shard_map/all_to_all | solution.py:74
  7.3 0.0 copy-done.3
  7.3 0.6 dynamic_slice.9
  7.9 9.1 %all-to-all-done.1 = bf16[128,8,256]{0,2,1:T(8,128)(2,1)S(1)} async-done(((bf16[128,8,256]{0,2,1:T(8,128)(2,1)}), bf16[128,8,256]{0,2,1:T(8,128)(2,1)S(1)}, u32[]{:S(2)}, u32[]{:S(2)}) %all-to-all-start.1) | async-done | bytes 524320 | tf_op jit(solution)/shard_map/all_to_all | solution.py:74
  17.0 0.1 convert_reduce_fusion.1
  17.1 1.4 %multiply_convert_fusion = (bf16[256]{0:T(256)(128)(2,1)S(1)}, f32[256]{0:T(256)S(1)}, f32[256]{0:T(256)S(1)}) fusion(f32[2048]{0:T(1024)} %param.7, s32[]{:T(128)S(6)} %select_n.15, f32[256]{0:T(256)S(1)} %convert_reduce_fusion.1, f32[2048]{0:T(1024)} %param.8, s32[]{:T(128)} %bitcast.6), kind=kLoop, calls=%fused_computation.72 | loop fusion | flops 1536 | bytes 5640 | tf_op jit(solution)/shard_map/convert_element_type | solution.py:82
  18.5 0.1 convert_bitcast_fusion
  18.6 0.3 copy.16
  19.0 0.0 copy-start.2
  19.0 0.1 fusion.4
  19.1 1.6 %collective-permute-start = (bf16[1025,128]{1,0:T(8,128)(2,1)S(1)}, bf16[1025,128]{1,0:T(8,128)(2,1)S(1)}, u32[]{:S(2)}, u32[]{:S(2)}) collective-permute-start(bf16[1025,128]{1,0:T(8,128)(2,1)S(1)} %get-tuple-element.11), channel_id=1, source_target_pairs={{0,1},{1,2},{2,3},{3,0},{4,5},{5,6},{6,7},{7,4},{8,9},{9,10},{10,1... | collective-permute-start | bytes 787208 | tf_op jit(solution)/shard_map/ppermute | solution.py:17
  20.8 2.2 %collective-permute-start.1 = (bf16[1025,128]{1,0:T(8,128)(2,1)S(1)}, bf16[1025,128]{1,0:T(8,128)(2,1)S(1)}, u32[]{:S(2)}, u32[]{:S(2)}) collective-permute-start(bf16[1025,128]{1,0:T(8,128)(2,1)S(1)} %get-tuple-element.12), channel_id=1, source_target_pairs={{1,0},{2,1},{3,2},{0,3},{5,4},{6,5},{7,6},{4,7},{9,8},{10,9},{11,1... | collective-permute-start | bytes 787208 | tf_op jit(solution)/shard_map/ppermute | solution.py:19
  23.0 0.0 copy-done.2
  23.0 1.1 %copy.21 = bf16[16,8,8,512]{3,2,0,1:T(8,128)(2,1)} copy(bf16[16,8,8,512]{3,2,1,0:T(8,128)(2,1)S(1)} %bitcast.86) | data formatting | bytes 2097152 | tf_op jit(solution)/shard_map/all_to_all | solution.py:73
  24.1 3.6 %all-to-all-start = ((bf16[128,8,512]{2,0,1:T(8,128)(2,1)}), bf16[128,8,512]{2,0,1:T(8,128)(2,1)S(1)}, u32[]{:S(2)}, u32[]{:S(2)}) async-start(bf16[128,8,512]{2,0,1:T(8,128)(2,1)} %bitcast.83), calls=%async_computation | async-start | bytes 2097152 | tf_op jit(solution)/shard_map/all_to_all | solution.py:73
  27.7 2.1 %collective-permute-done = bf16[1025,128]{1,0:T(8,128)(2,1)S(1)} collective-permute-done((bf16[1025,128]{1,0:T(8,128)(2,1)S(1)}, bf16[1025,128]{1,0:T(8,128)(2,1)S(1)}, u32[]{:S(2)}, u32[]{:S(2)}) %collective-permute-start) | collective-permute-done | bytes 262432 | tf_op jit(solution)/shard_map/ppermute | solution.py:17
  29.8 2.2 %collective-permute-done.1 = bf16[1025,128]{1,0:T(8,128)(2,1)S(1)} collective-permute-done((bf16[1025,128]{1,0:T(8,128)(2,1)S(1)}, bf16[1025,128]{1,0:T(8,128)(2,1)S(1)}, u32[]{:S(2)}, u32[]{:S(2)}) %collective-permute-start.1) | collective-permute-done | bytes 262432 | tf_op jit(solution)/shard_map/ppermute | solution.py:19
  32.0 0.1 pad_maximum_fusion
  32.1 0.0 copy-start
  32.1 0.8 abs_reduce_fusion
  32.9 0.2 copy-done
  33.1 0.7 reduce_max.9
  34.4 0.1 fusion.26
  34.5 0.2 multiply_reduce_fusion
  34.7 0.7 fusion.35
  35.4 0.7 fusion.34
  36.1 0.7 broadcast_multiply_fusion.7
  36.8 4.4 %broadcast_multiply_fusion.8 = (f32[1,512]{1,0:T(1,128)S(1)}, f32[1,512]{1,0:T(1,128)S(1)}, f32[1,512]{1,0:T(1,128)S(1)}, f32[1,512]{1,0:T(1,128)S(1)}, f32[1,51...) fusion(f32[1,512]{1,0:T(1,128)S(1)} %get-tuple-element.8, f32[]{:T(128)} %bitcast.7, f32[]{:T(128)} %bitcast.19, ...), kind=kLoop, calls=%fused_computation.71 | loop fusion | flops 3584 | bytes 16412 | tf_op jit(solution)/shard_map/mul | solution.py:56
  41.2 0.9 %fusion.23 = f32[1,512]{1,0:T(1,128)S(1)} fusion(f32[1,512]{1,0:T(1,128)S(1)} %get-tuple-element.19, f32[512,512]{0,1:T(8,128)S(1)} %get-tuple-element.38, f32[]{:T(128)S(6)} %mul.339), kind=kOutput, calls=%fused_computation.51 | convolution fusion | flops 4194304 | bytes 1052676 | tf_op jit(solution)/shard_map/dot_general | solution.py:52
  42.1 1.0 %fusion.32 = f32[1,512]{1,0:T(1,128)S(1)} fusion(f32[512,1]{0,1:T(1,128)S(1)} %bitcast.88, f32[512,512]{0,1:T(8,128)S(1)} %get-tuple-element.38, f32[]{:T(128)S(6)} %mul.339), kind=kOutput, calls=%fused_computation.87 | convolution fusion | flops 4194304 | bytes 1052676 | tf_op jit(solution)/shard_map/dot_general | solution.py:52
  43.1 1.0 %fusion.31 = f32[1,512]{1,0:T(1,128)S(1)} fusion(f32[512,1]{0,1:T(1,128)S(1)} %bitcast.91, f32[512,512]{0,1:T(8,128)S(1)} %get-tuple-element.38, f32[]{:T(128)S(6)} %mul.339), kind=kOutput, calls=%fused_computation.86 | convolution fusion | flops 4194304 | bytes 1052676 | tf_op jit(solution)/shard_map/dot_general | solution.py:52
  44.1 1.0 %fusion.30 = f32[1,512]{1,0:T(1,128)S(1)} fusion(f32[512,1]{0,1:T(1,128)S(1)} %bitcast.92, f32[512,512]{0,1:T(8,128)S(1)} %get-tuple-element.38, f32[]{:T(128)S(6)} %mul.339), kind=kOutput, calls=%fused_computation.85 | convolution fusion | flops 4194304 | bytes 1052676 | tf_op jit(solution)/shard_map/dot_general | solution.py:52
  45.1 1.0 %fusion.29 = f32[1,512]{1,0:T(1,128)S(1)} fusion(f32[512,1]{0,1:T(1,128)S(1)} %bitcast.90, f32[512,512]{0,1:T(8,128)S(1)} %get-tuple-element.38, f32[]{:T(128)S(6)} %mul.339), kind=kOutput, calls=%fused_computation.84 | convolution fusion | flops 4194304 | bytes 1052676 | tf_op jit(solution)/shard_map/dot_general | solution.py:52
  46.0 1.0 %fusion.28 = f32[1,512]{1,0:T(1,128)S(1)} fusion(f32[512,1]{0,1:T(1,128)S(1)} %bitcast.89, f32[512,512]{0,1:T(8,128)S(1)} %get-tuple-element.38, f32[]{:T(128)S(6)} %mul.339), kind=kOutput, calls=%fused_computation.83 | convolution fusion | flops 4194304 | bytes 1052676 | tf_op jit(solution)/shard_map/dot_general | solution.py:52
  47.0 1.0 %fusion.27 = f32[1,512]{1,0:T(1,128)S(1)} fusion(f32[512,1]{0,1:T(1,128)S(1)} %bitcast.99, f32[512,512]{0,1:T(8,128)S(1)} %get-tuple-element.38, f32[]{:T(128)S(6)} %mul.339), kind=kOutput, calls=%fused_computation.82 | convolution fusion | flops 4194304 | bytes 1052676 | tf_op jit(solution)/shard_map/dot_general | solution.py:56
  48.0 0.0 all-to-all-done
  48.0 0.2 convert_reduce_fusion
  48.2 0.0 copy-start.1
  48.2 0.2 fusion
  48.4 1.0 %copy-done.1 = bf16[1025,512]{1,0:T(8,128)(2,1)S(1)} copy-done((bf16[1025,512]{1,0:T(8,128)(2,1)S(1)}, bf16[1025,512]{1,0:T(8,128)(2,1)}, u32[]{:S(2)}) %copy-start.1) | copy-done | bytes 1049624
  49.4 0.7 fusion.15
  50.2 1.0 %fusion.36 = f32[1,512]{1,0:T(1,128)S(1)} fusion(f32[512,512]{1,0:T(8,128)S(1)} %fusion.15, f32[512,1]{0,1:T(1,128)S(1)} %bitcast.96), kind=kOutput, calls=%fused_computation.90 | convolution fusion | flops 3145728 | bytes 1052672 | tf_op jit(solution)/shard_map/dot_general | solution.py:96
  51.2 3.2 %multiply_add_fusion = f32[512,512]{1,0:T(8,128)S(1)} fusion(f32[512,512]{1,0:T(8,128)S(1)} %fusion.15, f32[]{:T(128)} %bitcast.46, f32[]{:T(128)} %bitcast.45, f32[512,512]{0,1:T(8,128)S(1)} %get-tuple-element.38, f32[]{:T(128)S(6)} %mul.339), kind=kOutput, calls=%fused_computation.27 | convolution fusion | flops 1612709888 | bytes 3145740 | tf_op jit(solution)/shard_map/dot_general | solution.py:52
  54.4 1.9 %convolution_multiply_fusion.4 = f32[512,512]{1,0:T(8,128)S(1)} fusion(f32[512,512]{1,0:T(8,128)S(1)} %multiply_add_fusion, f32[512,512]{0,1:T(8,128)S(1)} %get-tuple-element.38, f32[]{:T(128)S(6)} %mul.339), kind=kOutput, calls=%fused_computation.10 | convolution fusion | flops 1611923456 | bytes 3145732 | tf_op jit(solution)/shard_map/dot_general | solution.py:52
  56.3 4.1 %add_subtract_fusion.2 = f32[512,512]{1,0:T(8,128)S(1)} fusion(f32[512,512]{1,0:T(8,128)S(1)} %multiply_add_fusion, f32[512,512]{1,0:T(8,128)S(1)} %fusion.15, f32[512,512]{1,0:T(8,128)S(1)} %convolution_multiply_fusion.4, f32[]{:T(128)} %bitcast.46, f32[]{:T(128)} %bitcast.44, f32[]{:T(128)} %bitcast.43, f32[512,512]{0,1:T(8,128)S(1)} %get-tuple-element.38, ...), kind=kOutput, calls=%fused_computation.25 | convolution fusion | flops 1613758464 | bytes 5242896 | tf_op jit(solution)/shard_map/dot_general | solution.py:52
  60.4 3.9 %add_subtract_fusion.1 = f32[512,512]{1,0:T(8,128)S(1)} fusion(f32[512,512]{1,0:T(8,128)S(1)} %fusion.15, f32[512,512]{1,0:T(8,128)S(1)} %convolution_multiply_fusion.4, f32[512,512]{1,0:T(8,128)S(1)} %add_subtract_fusion.2, f32[]{:T(128)} %bitcast.46, f32[]{:T(128)} %bitcast.44, f32[]{:T(128)} %bitcast.42, f32[512,512]{0,1:T(8,128)S(1)} %get-tuple-element.38, ...), kind=kOutput, calls=%fused_computation.24 | convolution fusion | flops 1613758464 | bytes 5242896 | tf_op jit(solution)/shard_map/dot_general | solution.py:52
  64.3 2.6 %add_subtract_fusion = f32[512,512]{1,0:T(8,128)S(1)} fusion(f32[512,512]{1,0:T(8,128)S(1)} %add_subtract_fusion.2, f32[512,512]{1,0:T(8,128)S(1)} %fusion.15, f32[512,512]{1,0:T(8,128)S(1)} %add_subtract_fusion.1, f32[]{:T(128)} %bitcast.41, f32[512,512]{0,1:T(8,128)S(1)} %get-tuple-element.38, f32[]{:T(128)S(6)} %mul.339), kind=kOutput, calls=%fused_computation.23 | convolution fusion | flops 1612709888 | bytes 5242888 | tf_op jit(solution)/shard_map/dot_general | solution.py:52
  66.9 1.9 %convolution_multiply_fusion = f32[512,512]{1,0:T(8,128)S(1)} fusion(f32[512,512]{1,0:T(8,128)S(1)} %add_subtract_fusion, f32[512,512]{0,1:T(8,128)S(1)} %get-tuple-element.38, f32[]{:T(128)S(6)} %mul.339), kind=kOutput, calls=%fused_computation.6 | convolution fusion | flops 1611923456 | bytes 3145732 | tf_op jit(solution)/shard_map/dot_general | solution.py:52
  68.8 2.6 %fusion.5 = f32[512,512]{1,0:T(8,128)S(1)} fusion(f32[512,512]{1,0:T(8,128)S(1)} %add_subtract_fusion.1, f32[512,512]{1,0:T(8,128)S(1)} %convolution_multiply_fusion, f32[512,512]{1,0:T(8,128)S(1)} %fusion.15, f32[]{:T(128)} %bitcast.40, f32[512,512]{0,1:T(8,128)S(1)} %get-tuple-element.38, f32[]{:T(128)S(6)} %mul.339), kind=kOutput, calls=%fused_computation.20 | convolution fusion | flops 1612447744 | bytes 5242888 | tf_op jit(solution)/shard_map/dot_general | solution.py:56
  71.4 1.4 %fusion.2 = bf16[1024,512]{1,0:T(8,128)(2,1)S(1)} fusion(bf16[128,8,512]{2,0,1:T(8,128)(2,1)S(1)} %all-to-all-done, f32[512]{0:T(512)S(1)} %broadcast_multiply_fusion, bf16[1025,512]{1,0:T(8,128)(2,1)S(1)} %copy-done.1, f32[512,512]{1,0:T(8,128)S(1)} %add_subtract_fusion, f32[512,512]{1,0:T(8,128)S(1)} %fusion.5, f32[512,512]{1,0:T(8,128)S(1)} %fusion.15, ...), kind=kOutput, calls=%fused_computation.5 | convolution fusion | flops 540540928 | bytes 6293508 | tf_op jit(solution)/shard_map/dot_general | solution.py:97
  72.9 19.5 %all_to_all.45 = bf16[8,128,512]{2,1,0:T(8,128)(2,1)S(1)} all-to-all(bf16[8,128,512]{2,1,0:T(8,128)(2,1)S(1)} %bitcast.85), channel_id=1, replica_groups=mesh['mem'=8,'patch'=4] {'mem'}, dimensions={0} | all-to-all | bytes 2097152 | tf_op jit(solution)/shard_map/all_to_all | solution.py:101
  92.3 1.1 %copy.19 = bf16[8,16,8,512]{3,2,0,1:T(8,128)(2,1)} copy(bf16[8,16,8,512]{3,2,1,0:T(8,128)(2,1)S(1)} %bitcast.84) | data formatting | bytes 2097152 | tf_op jit(solution)/shard_map/all_to_all | solution.py:101
  (14 shorter events, 0.1 us)
Async XLA Ops:
  0.0 7.3 %copy-start.3 = (s32[8]{0:T(128)S(1)}, s32[8]{0:T(128)}, u32[]{:S(2)}) copy-start(s32[8]{0:T(128)} %param.9) | copy-start | bytes 100
  2.1 14.9 %all-to-all-start.1 = ((bf16[128,8,256]{0,2,1:T(8,128)(2,1)}), bf16[128,8,256]{0,2,1:T(8,128)(2,1)S(1)}, u32[]{:S(2)}, u32[]{:S(2)}) async-start(bf16[128,8,256]{0,2,1:T(8,128)(2,1)} %bitcast.3), calls=%async_computation.1 | async-start | bytes 1048576 | tf_op jit(solution)/shard_map/all_to_all | solution.py:74
  19.0 4.1 %copy-start.2 = (bf16[128,4096]{1,0:T(8,128)(2,1)S(1)}, bf16[128,4096]{1,0:T(8,128)(2,1)}, u32[]{:S(2)}) copy-start(bf16[128,4096]{1,0:T(8,128)(2,1)} %param.5) | copy-start | bytes 3145732
  19.1 10.6 %collective-permute-start = (bf16[1025,128]{1,0:T(8,128)(2,1)S(1)}, bf16[1025,128]{1,0:T(8,128)(2,1)S(1)}, u32[]{:S(2)}, u32[]{:S(2)}) collective-permute-start(bf16[1025,128]{1,0:T(8,128)(2,1)S(1)} %get-tuple-element.11), channel_id=1, source_target_pairs={{0,1},{1,2},{2,3},{3,0},{4,5},{5,6},{6,7},{7,4},{8,9},{9,10},{10,1... | collective-permute-start | bytes 787208 | tf_op jit(solution)/shard_map/ppermute | solution.py:17
  20.8 11.2 %collective-permute-start.1 = (bf16[1025,128]{1,0:T(8,128)(2,1)S(1)}, bf16[1025,128]{1,0:T(8,128)(2,1)S(1)}, u32[]{:S(2)}, u32[]{:S(2)}) collective-permute-start(bf16[1025,128]{1,0:T(8,128)(2,1)S(1)} %get-tuple-element.12), channel_id=1, source_target_pairs={{1,0},{2,1},{3,2},{0,3},{5,4},{6,5},{7,6},{4,7},{9,8},{10,9},{11,1... | collective-permute-start | bytes 787208 | tf_op jit(solution)/shard_map/ppermute | solution.py:19
  24.1 23.9 %all-to-all-start = ((bf16[128,8,512]{2,0,1:T(8,128)(2,1)}), bf16[128,8,512]{2,0,1:T(8,128)(2,1)S(1)}, u32[]{:S(2)}, u32[]{:S(2)}) async-start(bf16[128,8,512]{2,0,1:T(8,128)(2,1)} %bitcast.83), calls=%async_computation | async-start | bytes 2097152 | tf_op jit(solution)/shard_map/all_to_all | solution.py:73
  32.1 1.0 %copy-start = (bf16[1025,512]{1,0:T(8,128)(2,1)}, bf16[1025,512]{1,0:T(8,128)(2,1)S(1)}, u32[]{:S(2)}) copy-start(bf16[1025,512]{1,0:T(8,128)(2,1)S(1)} %pad_maximum_fusion) | copy-start | bytes 3148804
  48.2 1.2 %copy-start.1 = (bf16[1025,512]{1,0:T(8,128)(2,1)S(1)}, bf16[1025,512]{1,0:T(8,128)(2,1)}, u32[]{:S(2)}) copy-start(bf16[1025,512]{1,0:T(8,128)(2,1)} %copy-done) | copy-start | bytes 3148804
where the time goes:
time: 94 us; the launch traced here: 93.4 us
  matrix products  30.8 us (33%)
  blocking collectives  19.5 us (21%)
  waiting for transfers between devices  13.4 us (14%)
  starting transfers between devices  12.6 us (13%)
  other arithmetic  8.41 us (9%)
  local copies, waits for them, and re-layouts  7.73 us (8%)
    dot_general x14, matrix products, clenshaw(): jnp.dot(nearer, matrix, precision=lax.Precision.HIGHEST)  26.9 us
    all_to_all x1, blocking collectives, on_device(): lax.all_to_all(analysed, 'mem', split_axis=0, concat_axis=1, tiled=True)  19.5 us
    all_to_all x1, waiting for transfers between devices, on_device(): lax.all_to_all(obs_ens, 'mem', split_axis=1, concat_axis=0, tiled=True)  9.09 us
    all_to_all x1, starting transfers between devices, on_device(): lax.all_to_all(obs_ens, 'mem', split_axis=1, concat_axis=0, tiled=True)  5.2 us
    mul x1, other arithmetic, clenshaw(): coefs[0] * block + jnp.dot(nearer, matrix, precision=lax.Precision.HIGHEST)  4.4 us
    all_to_all x1, starting transfers between devices, on_device(): lax.all_to_all(state, 'mem', split_axis=1, concat_axis=0, tiled=True)  3.56 us
    unnamed x9, local copies, waits for them, and re-layouts  3.27 us
    ppermute x1, starting transfers between devices, extended(): lax.ppermute(head, axis, [((i + 1) % count, i) for i in range(count)])  2.25 us
  transfers between devices with their start and end apart: 4, of which 3 were waited for; matrix products, arithmetic and copies ran while one was open for 18% of the time, Pallas kernels for 0%

commit v1 on v0

--- a/solution.py
+++ b/solution.py
@@ -71,7 +71,15 @@
     count = lax.dynamic_slice_in_dim(counts, mem_index, 1, 0)[0]
     region_state, region_obs = (
         lax.all_to_all(state, "mem", split_axis=1, concat_axis=0, tiled=True),
-        lax.all_to_all(obs_ens, "mem", split_axis=1, concat_axis=0, tiled=True),
+        jnp.concatenate(
+            lax.all_to_all(
+                jnp.stack(jnp.split(obs_ens, lax.axis_size("mem"), axis=1)),
+                "mem",
+                split_axis=0,
+                concat_axis=0,
+            ),
+            axis=0,
+        ),
     )
     members = region_obs.shape[0]
     full_obs = region_obs.astype(jnp.float32)

time: 94 us -> 104 us (1.11)
  local copies, waits for them, and re-layouts: 7.73 us -> 17.1 us
    unnamed x9 -> x15, local copies, waits for them, and re-layouts: 3.27 us -> 11.5 us
    another operation x0 -> x1, local copies, waits for them, and re-layouts: none -> 1.47 us  [on_device(): jnp.stack(jnp.split(obs_ens, lax.axis_size('mem'), axis=1))]
  transfers between devices with their start and end apart: 4 -> 4, of which waited for: 3 -> 3; matrix products, arithmetic and copies ran while one was open for 18% -> 16% of each run, Pallas kernels for 0% -> 0%
where the time goes in v1:
time: 104 us; the launch traced here: 103 us
  matrix products  30.9 us (30%)
  blocking collectives  19.4 us (19%)
  local copies, waits for them, and re-layouts  17.1 us (16%)
  waiting for transfers between devices  13.4 us (13%)
  starting transfers between devices  12.6 us (12%)
  other arithmetic  8.36 us (8%)
    dot_general x14, matrix products, clenshaw(): jnp.dot(nearer, matrix, precision=lax.Precision.HIGHEST)  26.9 us
    all_to_all x1, blocking collectives, on_device(): lax.all_to_all(analysed, 'mem', split_axis=0, concat_axis=1, tiled=True)  19.4 us
    unnamed x15, local copies, waits for them, and re-layouts  11.5 us
    all_to_all x1, waiting for transfers between devices, on_device(): lax.all_to_all(jnp.stack(jnp.split(obs_ens, lax.axis_size('mem'), axis=1)...  9.09 us
    all_to_all x1, starting transfers between devices, on_device(): lax.all_to_all(jnp.stack(jnp.split(obs_ens, lax.axis_size('mem'), axis=1)...  5.2 us
    mul x1, other arithmetic, clenshaw(): coefs[0] * block + jnp.dot(nearer, matrix, precision=lax.Precision.HIGHEST)  4.4 us
    all_to_all x1, starting transfers between devices, on_device(): lax.all_to_all(state, 'mem', split_axis=1, concat_axis=0, tiled=True)  3.56 us
    ppermute x1, starting transfers between devices, extended(): lax.ppermute(head, axis, [((i + 1) % count, i) for i in range(count)])  2.25 us
  transfers between devices with their start and end apart: 4, of which 3 were waited for; matrix products, arithmetic and copies ran while one was open for 16% of the time, Pallas kernels for 0%

profile of v1, /device:TPU:0, one launch (start us, length us, event | category | flops | bytes accessed | tf_op | source)
XLA Modules:
  0.0 102.7 jit_solution(5401994295244682768)
XLA Ops:
  0.0 0.0 copy-start.3
  0.0 1.5 %bitcast_dynamic-update-slice_fusion.7 = bf16[8,128,256]{2,1,0:T(8,128)(2,1)} fusion(bf16[128,2048]{1,0:T(8,128)(2,1)} %param.6), kind=kLoop, calls=%fused_computation.53 | loop fusion | bytes 131072
  1.5 1.5 %bitcast_dynamic-update-slice_fusion.6 = bf16[8,128,256]{2,1,0:T(8,128)(2,1)} fusion(bf16[8,128,256]{2,1,0:T(8,128)(2,1)} %bitcast_dynamic-update-slice_fusion.7, bf16[128,2048]{1,0:T(8,128)(2,1)} %param.6), kind=kLoop, calls=%fused_computation.52 | loop fusion | bytes 131072
  3.0 1.5 %bitcast_dynamic-update-slice_fusion.5 = bf16[8,128,256]{2,1,0:T(8,128)(2,1)} fusion(bf16[8,128,256]{2,1,0:T(8,128)(2,1)} %bitcast_dynamic-update-slice_fusion.6, bf16[128,2048]{1,0:T(8,128)(2,1)} %param.6), kind=kLoop, calls=%fused_computation.51 | loop fusion | bytes 131072
  4.4 1.5 %bitcast_dynamic-update-slice_fusion.4 = bf16[8,128,256]{2,1,0:T(8,128)(2,1)} fusion(bf16[8,128,256]{2,1,0:T(8,128)(2,1)} %bitcast_dynamic-update-slice_fusion.5, bf16[128,2048]{1,0:T(8,128)(2,1)} %param.6), kind=kLoop, calls=%fused_computation.50 | loop fusion | bytes 131072
  5.9 1.5 %bitcast_dynamic-update-slice_fusion.3 = bf16[8,128,256]{2,1,0:T(8,128)(2,1)} fusion(bf16[8,128,256]{2,1,0:T(8,128)(2,1)} %bitcast_dynamic-update-slice_fusion.4, bf16[128,2048]{1,0:T(8,128)(2,1)} %param.6), kind=kLoop, calls=%fused_computation.49 | loop fusion | bytes 131072
  7.4 1.5 %bitcast_dynamic-update-slice_fusion.2 = bf16[8,128,256]{2,1,0:T(8,128)(2,1)} fusion(bf16[8,128,256]{2,1,0:T(8,128)(2,1)} %bitcast_dynamic-update-slice_fusion.3, bf16[128,2048]{1,0:T(8,128)(2,1)} %param.6), kind=kLoop, calls=%fused_computation.48 | loop fusion | bytes 131072
  8.9 1.5 %bitcast_dynamic-update-slice_fusion.1 = bf16[8,128,256]{2,1,0:T(8,128)(2,1)} fusion(bf16[8,128,256]{2,1,0:T(8,128)(2,1)} %bitcast_dynamic-update-slice_fusion.2, bf16[128,2048]{1,0:T(8,128)(2,1)} %param.6), kind=kLoop, calls=%fused_computation.47 | loop fusion | bytes 131072
  10.3 1.5 %bitcast_dynamic-update-slice_fusion = bf16[8,128,256]{2,1,0:T(8,128)(2,1)} fusion(bf16[8,128,256]{2,1,0:T(8,128)(2,1)} %bitcast_dynamic-update-slice_fusion.1, bf16[128,2048]{1,0:T(8,128)(2,1)} %param.6), kind=kLoop, calls=%fused_computation.46 | loop fusion | bytes 131072 | tf_op jit(solution)/shard_map/stack | solution.py:76
  11.8 5.2 %all-to-all-start.1 = ((bf16[8,128,256]{2,1,0:T(8,128)(2,1)}), bf16[8,128,256]{2,1,0:T(8,128)(2,1)S(1)}, u32[]{:S(2)}, u32[]{:S(2)}) async-start(bf16[8,128,256]{2,1,0:T(8,128)(2,1)} %bitcast_dynamic-update-slice_fusion), calls=%async_computation.1 | async-start | bytes 1048576 | tf_op jit(solution)/shard_map/all_to_all | solution.py:75
  17.0 0.0 copy-done.3
  17.0 0.6 dynamic_slice.9
  17.6 9.1 %all-to-all-done.1 = bf16[8,128,256]{2,1,0:T(8,128)(2,1)S(1)} async-done(((bf16[8,128,256]{2,1,0:T(8,128)(2,1)}), bf16[8,128,256]{2,1,0:T(8,128)(2,1)S(1)}, u32[]{:S(2)}, u32[]{:S(2)}) %all-to-all-start.1) | async-done | bytes 524320 | tf_op jit(solution)/shard_map/all_to_all | solution.py:75
  26.7 0.2 convert_reduce_fusion.1
  26.9 1.4 %multiply_convert_fusion = (bf16[256]{0:T(256)(128)(2,1)S(1)}, f32[256]{0:T(256)S(1)}, f32[256]{0:T(256)S(1)}) fusion(f32[2048]{0:T(1024)} %param.7, s32[]{:T(128)S(6)} %select_n.15, f32[256]{0:T(256)S(1)} %convert_reduce_fusion.1, f32[2048]{0:T(1024)} %param.8, s32[]{:T(128)} %bitcast.12), kind=kLoop, calls=%fused_computation.79 | loop fusion | flops 1536 | bytes 5640 | tf_op jit(solution)/shard_map/convert_element_type | solution.py:90
  28.3 0.0 copy-start.2
  28.3 0.1 fusion.4
  28.5 1.6 %collective-permute-start = (bf16[1025,128]{1,0:T(8,128)(2,1)S(1)}, bf16[1025,128]{1,0:T(8,128)(2,1)S(1)}, u32[]{:S(2)}, u32[]{:S(2)}) collective-permute-start(bf16[1025,128]{1,0:T(8,128)(2,1)S(1)} %get-tuple-element.11), channel_id=1, source_target_pairs={{0,1},{1,2},{2,3},{3,0},{4,5},{5,6},{6,7},{7,4},{8,9},{9,10},{10,1... | collective-permute-start | bytes 787208 | tf_op jit(solution)/shard_map/ppermute | solution.py:17
  30.1 2.2 %collective-permute-start.1 = (bf16[1025,128]{1,0:T(8,128)(2,1)S(1)}, bf16[1025,128]{1,0:T(8,128)(2,1)S(1)}, u32[]{:S(2)}, u32[]{:S(2)}) collective-permute-start(bf16[1025,128]{1,0:T(8,128)(2,1)S(1)} %get-tuple-element.12), channel_id=1, source_target_pairs={{1,0},{2,1},{3,2},{0,3},{5,4},{6,5},{7,6},{4,7},{9,8},{10,9},{11,1... | collective-permute-start | bytes 787208 | tf_op jit(solution)/shard_map/ppermute | solution.py:19
  32.4 0.0 copy-done.2
  32.4 1.1 %copy.13 = bf16[16,8,8,512]{3,2,0,1:T(8,128)(2,1)} copy(bf16[16,8,8,512]{3,2,1,0:T(8,128)(2,1)S(1)} %bitcast.99) | data formatting | bytes 2097152 | tf_op jit(solution)/shard_map/all_to_all | solution.py:73
  33.4 3.6 %all-to-all-start = ((bf16[128,8,512]{2,0,1:T(8,128)(2,1)}), bf16[128,8,512]{2,0,1:T(8,128)(2,1)S(1)}, u32[]{:S(2)}, u32[]{:S(2)}) async-start(bf16[128,8,512]{2,0,1:T(8,128)(2,1)} %bitcast.96), calls=%async_computation | async-start | bytes 2097152 | tf_op jit(solution)/shard_map/all_to_all | solution.py:73
  37.0 2.1 %collective-permute-done = bf16[1025,128]{1,0:T(8,128)(2,1)S(1)} collective-permute-done((bf16[1025,128]{1,0:T(8,128)(2,1)S(1)}, bf16[1025,128]{1,0:T(8,128)(2,1)S(1)}, u32[]{:S(2)}, u32[]{:S(2)}) %collective-permute-start) | collective-permute-done | bytes 262432 | tf_op jit(solution)/shard_map/ppermute | solution.py:17
  39.1 2.2 %collective-permute-done.1 = bf16[1025,128]{1,0:T(8,128)(2,1)S(1)} collective-permute-done((bf16[1025,128]{1,0:T(8,128)(2,1)S(1)}, bf16[1025,128]{1,0:T(8,128)(2,1)S(1)}, u32[]{:S(2)}, u32[]{:S(2)}) %collective-permute-start.1) | collective-permute-done | bytes 262432 | tf_op jit(solution)/shard_map/ppermute | solution.py:19
  41.3 0.1 pad_maximum_fusion
  41.5 0.0 copy-start
  41.5 0.8 abs_reduce_fusion
  42.2 0.2 copy-done
  42.4 0.7 reduce_max.9
  43.7 0.1 fusion.26
  43.9 0.2 multiply_reduce_fusion
  44.1 0.7 fusion.35
  44.8 0.7 fusion.34
  45.4 0.7 broadcast_multiply_fusion.7
  46.1 4.4 %broadcast_multiply_fusion.8 = (f32[1,512]{1,0:T(1,128)S(1)}, f32[1,512]{1,0:T(1,128)S(1)}, f32[1,512]{1,0:T(1,128)S(1)}, f32[1,512]{1,0:T(1,128)S(1)}, f32[1,51...) fusion(f32[1,512]{1,0:T(1,128)S(1)} %get-tuple-element.8, f32[]{:T(128)} %bitcast.13, f32[]{:T(128)} %bitcast.25, ...), kind=kLoop, calls=%fused_computation.78 | loop fusion | flops 3584 | bytes 16412 | tf_op jit(solution)/shard_map/mul | solution.py:56
  50.5 0.9 fusion.23
  51.5 1.0 fusion.32
  52.5 1.0 fusion.31
  53.4 1.0 fusion.30
  54.4 1.0 fusion.29
  55.4 1.0 fusion.28
  56.4 1.0 fusion.27
  57.3 0.0 all-to-all-done
  57.4 0.2 convert_reduce_fusion
  57.6 0.0 copy-start.1
  57.6 0.2 fusion
  57.8 1.0 copy-done.1
  58.8 0.7 fusion.15
  59.5 1.0 fusion.36
  60.5 3.2 %multiply_add_fusion = f32[512,512]{1,0:T(8,128)S(1)} fusion(f32[512,512]{1,0:T(8,128)S(1)} %fusion.15, f32[]{:T(128)} %bitcast.52, f32[]{:T(128)} %bitcast.51, f32[512,512]{0,1:T(8,128)S(1)} %get-tuple-element.38, f32[]{:T(128)S(6)} %mul.339), kind=kOutput, calls=%fused_computation.25 | convolution fusion | flops 1612709888 | bytes 3145740 | tf_op jit(solution)/shard_map/dot_general | solution.py:52
  63.7 1.9 %convolution_multiply_fusion.4 = f32[512,512]{1,0:T(8,128)S(1)} fusion(f32[512,512]{1,0:T(8,128)S(1)} %multiply_add_fusion, f32[512,512]{0,1:T(8,128)S(1)} %get-tuple-element.38, f32[]{:T(128)S(6)} %mul.339), kind=kOutput, calls=%fused_computation.10 | convolution fusion | flops 1611923456 | bytes 3145732 | tf_op jit(solution)/shard_map/dot_general | solution.py:52
  65.6 4.1 %add_subtract_fusion.2 = f32[512,512]{1,0:T(8,128)S(1)} fusion(f32[512,512]{1,0:T(8,128)S(1)} %multiply_add_fusion, f32[512,512]{1,0:T(8,128)S(1)} %fusion.15, f32[512,512]{1,0:T(8,128)S(1)} %convolution_multiply_fusion.4, f32[]{:T(128)} %bitcast.52, f32[]{:T(128)} %bitcast.50, f32[]{:T(128)} %bitcast.49, f32[512,512]{0,1:T(8,128)S(1)} %get-tuple-element.38, ...), kind=kOutput, calls=%fused_computation.23 | convolution fusion | flops 1613758464 | bytes 5242896 | tf_op jit(solution)/shard_map/dot_general | solution.py:52
  69.8 3.9 %add_subtract_fusion.1 = f32[512,512]{1,0:T(8,128)S(1)} fusion(f32[512,512]{1,0:T(8,128)S(1)} %fusion.15, f32[512,512]{1,0:T(8,128)S(1)} %convolution_multiply_fusion.4, f32[512,512]{1,0:T(8,128)S(1)} %add_subtract_fusion.2, f32[]{:T(128)} %bitcast.52, f32[]{:T(128)} %bitcast.50, f32[]{:T(128)} %bitcast.48, f32[512,512]{0,1:T(8,128)S(1)} %get-tuple-element.38, ...), kind=kOutput, calls=%fused_computation.22 | convolution fusion | flops 1613758464 | bytes 5242896 | tf_op jit(solution)/shard_map/dot_general | solution.py:52
  73.7 2.6 %add_subtract_fusion = f32[512,512]{1,0:T(8,128)S(1)} fusion(f32[512,512]{1,0:T(8,128)S(1)} %add_subtract_fusion.2, f32[512,512]{1,0:T(8,128)S(1)} %fusion.15, f32[512,512]{1,0:T(8,128)S(1)} %add_subtract_fusion.1, f32[]{:T(128)} %bitcast.47, f32[512,512]{0,1:T(8,128)S(1)} %get-tuple-element.38, f32[]{:T(128)S(6)} %mul.339), kind=kOutput, calls=%fused_computation.21 | convolution fusion | flops 1612709888 | bytes 5242888 | tf_op jit(solution)/shard_map/dot_general | solution.py:52
  76.2 1.9 %convolution_multiply_fusion = f32[512,512]{1,0:T(8,128)S(1)} fusion(f32[512,512]{1,0:T(8,128)S(1)} %add_subtract_fusion, f32[512,512]{0,1:T(8,128)S(1)} %get-tuple-element.38, f32[]{:T(128)S(6)} %mul.339), kind=kOutput, calls=%fused_computation.6 | convolution fusion | flops 1611923456 | bytes 3145732 | tf_op jit(solution)/shard_map/dot_general | solution.py:52
  78.1 2.6 %fusion.5 = f32[512,512]{1,0:T(8,128)S(1)} fusion(f32[512,512]{1,0:T(8,128)S(1)} %add_subtract_fusion.1, f32[512,512]{1,0:T(8,128)S(1)} %convolution_multiply_fusion, f32[512,512]{1,0:T(8,128)S(1)} %fusion.15, f32[]{:T(128)} %bitcast.46, f32[512,512]{0,1:T(8,128)S(1)} %get-tuple-element.38, f32[]{:T(128)S(6)} %mul.339), kind=kOutput, calls=%fused_computation.18 | convolution fusion | flops 1612447744 | bytes 5242888 | tf_op jit(solution)/shard_map/dot_general | solution.py:56
  80.8 1.4 %fusion.2 = bf16[1024,512]{1,0:T(8,128)(2,1)S(1)} fusion(bf16[128,8,512]{2,0,1:T(8,128)(2,1)S(1)} %all-to-all-done, f32[512]{0:T(512)S(1)} %broadcast_multiply_fusion, bf16[1025,512]{1,0:T(8,128)(2,1)S(1)} %copy-done.1, f32[512,512]{1,0:T(8,128)S(1)} %add_subtract_fusion, f32[512,512]{1,0:T(8,128)S(1)} %fusion.5, f32[512,512]{1,0:T(8,128)S(1)} %fusion.15, ...), kind=kOutput, calls=%fused_computation.5 | convolution fusion | flops 540540928 | bytes 6293508 | tf_op jit(solution)/shard_map/dot_general | solution.py:105
  82.2 19.4 %all_to_all.37 = bf16[8,128,512]{2,1,0:T(8,128)(2,1)S(1)} all-to-all(bf16[8,128,512]{2,1,0:T(8,128)(2,1)S(1)} %bitcast.98), channel_id=1, replica_groups=mesh['mem'=8,'patch'=4] {'mem'}, dimensions={0} | all-to-all | bytes 2097152 | tf_op jit(solution)/shard_map/all_to_all | solution.py:109
  101.6 1.1 %copy.11 = bf16[8,16,8,512]{3,2,0,1:T(8,128)(2,1)} copy(bf16[8,16,8,512]{3,2,1,0:T(8,128)(2,1)S(1)} %bitcast.97) | data formatting | bytes 2097152 | tf_op jit(solution)/shard_map/all_to_all | solution.py:109
  (14 shorter events, 0.1 us)
Async XLA Ops:
  0.0 17.0 %copy-start.3 = (s32[8]{0:T(128)S(1)}, s32[8]{0:T(128)}, u32[]{:S(2)}) copy-start(s32[8]{0:T(128)} %param.9) | copy-start | bytes 100
  11.8 14.9 %all-to-all-start.1 = ((bf16[8,128,256]{2,1,0:T(8,128)(2,1)}), bf16[8,128,256]{2,1,0:T(8,128)(2,1)S(1)}, u32[]{:S(2)}, u32[]{:S(2)}) async-start(bf16[8,128,256]{2,1,0:T(8,128)(2,1)} %bitcast_dynamic-update-slice_fusion), calls=%async_computation.1 | async-start | bytes 1048576 | tf_op jit(solution)/shard_map/all_to_all | solution.py:75
  28.3 4.1 %copy-start.2 = (bf16[128,4096]{1,0:T(8,128)(2,1)S(1)}, bf16[128,4096]{1,0:T(8,128)(2,1)}, u32[]{:S(2)}) copy-start(bf16[128,4096]{1,0:T(8,128)(2,1)} %param.5) | copy-start | bytes 3145732
  28.5 10.6 %collective-permute-start = (bf16[1025,128]{1,0:T(8,128)(2,1)S(1)}, bf16[1025,128]{1,0:T(8,128)(2,1)S(1)}, u32[]{:S(2)}, u32[]{:S(2)}) collective-permute-start(bf16[1025,128]{1,0:T(8,128)(2,1)S(1)} %get-tuple-element.11), channel_id=1, source_target_pairs={{0,1},{1,2},{2,3},{3,0},{4,5},{5,6},{6,7},{7,4},{8,9},{9,10},{10,1... | collective-permute-start | bytes 787208 | tf_op jit(solution)/shard_map/ppermute | solution.py:17
  30.1 11.2 %collective-permute-start.1 = (bf16[1025,128]{1,0:T(8,128)(2,1)S(1)}, bf16[1025,128]{1,0:T(8,128)(2,1)S(1)}, u32[]{:S(2)}, u32[]{:S(2)}) collective-permute-start(bf16[1025,128]{1,0:T(8,128)(2,1)S(1)} %get-tuple-element.12), channel_id=1, source_target_pairs={{1,0},{2,1},{3,2},{0,3},{5,4},{6,5},{7,6},{4,7},{9,8},{10,9},{11,1... | collective-permute-start | bytes 787208 | tf_op jit(solution)/shard_map/ppermute | solution.py:19
  33.4 23.9 %all-to-all-start = ((bf16[128,8,512]{2,0,1:T(8,128)(2,1)}), bf16[128,8,512]{2,0,1:T(8,128)(2,1)S(1)}, u32[]{:S(2)}, u32[]{:S(2)}) async-start(bf16[128,8,512]{2,0,1:T(8,128)(2,1)} %bitcast.96), calls=%async_computation | async-start | bytes 2097152 | tf_op jit(solution)/shard_map/all_to_all | solution.py:73
  41.5 1.0 copy-start
  57.6 1.2 %copy-start.1 = (bf16[1025,512]{1,0:T(8,128)(2,1)S(1)}, bf16[1025,512]{1,0:T(8,128)(2,1)}, u32[]{:S(2)}) copy-start(bf16[1025,512]{1,0:T(8,128)(2,1)} %copy-done) | copy-start | bytes 3148804
